TPU v7x, 32 devices: a whole 2x2x4 slice. The times are simulated.
32 devices in a mesh: kpt: 2 (over x), grid: 16 (over z, y, core).
Axes of the slice: x: 2, y: 2, z: 4, core: 2. Of those that a mesh axis runs over, the one named last changes fastest.
Arguments:
- orbitals: bfloat16 [4, 2, 2, 512, 256, 256], P('kpt', None, None, 'grid'), may hold values from -6 to 6
- kweights: int32 [4], P('kpt'), may hold values from 1 to 16
- occupations: int32 [4, 2], P('kpt'), may hold values from 0 to 2
- z_basis: float32 [512, 512], replicated, may hold values from -0.25 to 0.25
- z_eigen: float32 [512], replicated, may hold values from 0.25 to 4
Outputs:
- potential: float32 [512, 256, 256], P('grid')
All inputs are finite; a program needn't handle non-finite values.
Results may differ from a plain program's by a relative error of at most 0.0003.
Values sent between devices are 32-bit elements; how exact they have to be, the bound alone decides.
A program may use at most 128 MiB of HBM per device.

v0:
```python
import jax
import jax.numpy as jnp
import numpy as np
from jax import lax
from jax.experimental import pallas as pl
from jax.experimental.pallas import tpu as pltpu
from jax.sharding import PartitionSpec as P


precise = lax.Precision.HIGH
CHUNKS = 4

MESH = pl.DeviceIdType.MESH
LANES = 128
TILE = 8
STEP = 2
AHEAD = 6
SLOTS = 3
SLACK = 4
bf16 = jnp.bfloat16
f32 = jnp.float32


def basis_tables(length):
    position = np.arange(length)
    angles = (position[:, None] * position[None, :] % length) * (2.0 * np.pi / length)
    table = np.where(position[:, None] <= length // 2, np.cos(angles), np.sin(angles))
    edges = (position == 0) | (position == length // 2)
    scaled = table * (np.where(edges, 1.0, 2.0) / length)[:, None]
    return table, scaled


def halves(table):
    high = table.astype(bf16)
    low = (table - high.astype(np.float64)).astype(bf16)
    return high, low


def split(value):
    high = value.astype(bf16)
    return high, (value - high.astype(f32)).astype(bf16)


def dot(left, right):
    return jnp.dot(left, right, preferred_element_type=f32)


def fused_kernel(
    orbitals, kweights, occupations, basis, eigen, forward_y, forward_x, inverse_x, wave_y, wave_x,
    half_out,
    block, rows, table_y, table_x, table_w, basis_rows, eigen_row, own, leaving, joined, leaped, column, projected,
    scaled_high, scaled_low, basis_high, basis_low, basis_turned, eigen_column, modes, half,
    load_sem, table_sem, x_send, x_recv, f_send, f_recv, b_send, b_recv, h_send, h_recv, h_keep,
):
    points, bands, parts, planes, nx, ny = orbitals.shape
    blocks = lax.axis_size("grid")
    step = leaving.shape[1]
    chunks = planes // step
    groups = planes // TILE
    ratio = TILE // step
    kxc = nx // blocks
    depth = blocks * TILE
    pairs = kxc // 2
    nz = basis.shape[0] * basis.shape[1]
    side = lax.axis_index("kpt")
    other = 1 - side
    me = lax.axis_index("grid")

    barrier = pltpu.get_barrier_semaphore()
    pl.semaphore_signal(barrier, inc=1, device_id={"kpt": other}, device_id_type=MESH)

    @pl.loop(1, blocks)
    def _(i):
        pl.semaphore_signal(barrier, inc=1, device_id={"grid": lax.rem(me + i, blocks)}, device_id_type=MESH)

    def load(c):
        slot = lax.rem(c, SLOTS)
        return pltpu.make_async_copy(
            orbitals.at[:, :, :, pl.ds(c * step, step)], block.at[slot], load_sem.at[slot]
        )

    for c in range(SLOTS):
        load(c).start()
    tables = [
        pltpu.make_async_copy(forward_y.at[other], table_y.at[:, pl.ds(0, LANES)], table_sem.at[0]),
        pltpu.make_async_copy(forward_y.at[side], table_y.at[:, pl.ds(LANES, LANES)], table_sem.at[1]),
        pltpu.make_async_copy(forward_x, table_x, table_sem.at[2]),
        pltpu.make_async_copy(inverse_x, table_w, table_sem.at[3]),
        pltpu.make_async_copy(basis, basis_rows, table_sem.at[4]),
        pltpu.make_async_copy(eigen, eigen_row, table_sem.at[5]),
    ]
    for copy in tables:
        copy.start()

    def send_x(c):
        return pltpu.make_async_remote_copy(
            src_ref=leaving.at[c], dst_ref=joined.at[c], send_sem=x_send.at[c], recv_sem=x_recv.at[c],
            device_id={"kpt": other}, device_id_type=MESH,
        )

    def density(c):
        slot = lax.rem(c, SLOTS)
        load(c).wait()
        strip = 32
        factors = [
            [(kweights[k] * occupations[k, b]).astype(f32) / (16.0 * points * bands) for b in range(bands)]
            for k in range(points)
        ]

        @pl.loop(0, step)
        def _(p):
            @pl.loop(0, nx // strip)
            def _(r):
                where = pl.ds(pl.multiple_of(r * strip, strip), strip)
                total = None
                for k in range(points):
                    for b in range(bands):
                        square = None
                        for part in range(parts):
                            value = block[slot, k, b, part, p, where, :].astype(f32)
                            square = value * value if square is None else square + value * value
                        term = factors[k][b] * square
                        total = term if total is None else total + term
                high, low = split(total)
                rows[where, pl.ds(0, ny)] = high
                rows[where, pl.ds(ny, ny)] = low

            line = dot(rows[...], table_y[pl.ds(0, 2 * ny), :]) + dot(
                rows[:, pl.ds(0, ny)], table_y[pl.ds(2 * ny, ny), :]
            )
            leaving[c, p] = line[:, :LANES]
            own[c, p] = line[:, LANES:]

        @pl.when(c + SLOTS < chunks)
        def _():
            load(c + SLOTS).start()

        send_x(c).start()

    def part_of(c, d):
        return pl.ds(pl.multiple_of((c * blocks + d) * (step * kxc), TILE), step * kxc)

    def place_of(c, d):
        first = ((c // ratio) * blocks + d) * TILE + lax.rem(c, ratio) * step
        return pl.ds(pl.multiple_of(first * kxc, TILE), step * kxc)

    def send_f(c, i):
        to = lax.rem(me + i, blocks)
        return pltpu.make_async_remote_copy(
            src_ref=leaped.at[part_of(c, to)], dst_ref=column.at[place_of(c, me)],
            send_sem=f_send.at[c], recv_sem=f_recv.at[c],
            device_id={"grid": to}, device_id_type=MESH,
        )

    def arrivals(sem):
        whole = column.at[pl.ds(0, (blocks - 1) * step * kxc)]
        return pltpu.make_async_copy(whole, whole, sem)

    def spectrum(c):
        send_x(c).wait_recv()

        @pl.loop(0, step // 2)
        def _(q):
            p = q * 2
            both = jnp.concatenate([own[c, p] + joined[c, p], own[c, p + 1] + joined[c, p + 1]], axis=1)
            high, low = split(both)
            result = dot(table_x[...], jnp.concatenate([high, high, low], axis=0))
            for s in range(2):
                for d in range(blocks):
                    first = ((c * blocks + d) * step + p + s) * kxc
                    leaped[pl.ds(pl.multiple_of(first, TILE), kxc), :] = result[
                        d * kxc : (d + 1) * kxc, s * LANES : (s + 1) * LANES
                    ]

        column[place_of(c, me), :] = leaped[part_of(c, me), :]

        @pl.loop(1, blocks)
        def _(i):
            send_f(c, i).start()

    def prepare():
        for copy in tables[4:]:
            copy.wait()

        @pl.loop(0, groups)
        def _(g):
            taken = basis_rows[:, pl.ds(pl.multiple_of(g * TILE, TILE), TILE), :].reshape(depth, nz)
            high, low = split(taken)
            basis_high[g] = high
            basis_low[g] = low
            high, low = split(taken.T)
            basis_turned[g, :, pl.ds(0, depth)] = high
            basis_turned[g, :, pl.ds(depth, depth)] = high
            basis_turned[g, :, pl.ds(2 * depth, depth)] = low

        eigen_column[...] = jnp.broadcast_to(eigen_row[...], (LANES, nz)).T

    def term(g, q):
        start = g * (depth * kxc) + 2 * q
        both = jnp.concatenate(
            [column[pl.ds(start, depth, stride=kxc), :], column[pl.ds(start + 1, depth, stride=kxc), :]], axis=1
        )
        high, low = split(both)
        return dot(basis_turned[g], jnp.concatenate([high, low, high], axis=0))

    def wait_f(g):
        for r in range(ratio):
            arrivals(f_recv.at[g * ratio + r]).wait()

    def gather(g):
        wait_f(g)

        @pl.loop(0, pairs)
        def _(q):
            @pl.when(g == 0)
            def _():
                projected[q] = term(g, q)

            @pl.when(g > 0)
            def _():
                projected[q] += term(g, q)

    def gather_last():
        g = groups - 1
        wait_f(g)
        across = wave_y[pl.ds(side, 1), :]

        @pl.loop(0, pairs)
        def _(q):
            total = term(g, q)
            if groups > 1:
                total = total + projected[q]
            for s in range(2):
                along = wave_x[me * kxc + 2 * q + s]
                value = total[:, s * LANES : (s + 1) * LANES] / (eigen_column[...] + (along + across))
                high, low = split(value)
                scaled_high[q, :, pl.ds(s * LANES, LANES)] = high
                scaled_low[q, :, pl.ds(s * LANES, LANES)] = low

    def send_b(c, i):
        to = lax.rem(me + i, blocks)
        return pltpu.make_async_remote_copy(
            src_ref=column.at[place_of(c, to)], dst_ref=modes.at[part_of(c, me)],
            send_sem=b_send.at[c], recv_sem=b_recv.at[c],
            device_id={"grid": to}, device_id_type=MESH,
        )

    def filtered(g):
        @pl.loop(0, pairs)
        def _(q):
            result = (
                dot(basis_high[g], scaled_high[q])
                + dot(basis_high[g], scaled_low[q])
                + dot(basis_low[g], scaled_high[q])
            )
            start = g * (depth * kxc) + 2 * q
            column[pl.ds(start, depth, stride=kxc), :] = result[:, :LANES]
            column[pl.ds(start + 1, depth, stride=kxc), :] = result[:, LANES:]

        for r in range(ratio):
            @pl.loop(1, blocks)
            def _(i):
                send_b(g * ratio + r, i).start()

        for r in range(ratio):
            modes[part_of(g * ratio + r, me), :] = column[place_of(g * ratio + r, me), :]

    def send_h(c):
        return pltpu.make_async_remote_copy(
            src_ref=half.at[c], dst_ref=half_out.at[side, pl.ds(c * step, step)],
            send_sem=h_send.at[c], recv_sem=h_recv.at[c],
            device_id={"kpt": other}, device_id_type=MESH,
        )

    def keep_h(c):
        return pltpu.make_async_copy(half.at[c], half_out.at[side, pl.ds(c * step, step)], h_keep.at[c])

    def inverse(c):
        arrivals(b_recv.at[c]).wait()

        @pl.loop(0, step // 2)
        def _(q):
            p = q * 2
            both = jnp.concatenate(
                [
                    jnp.concatenate(
                        [
                            modes[pl.ds(pl.multiple_of(((c * blocks + d) * step + p + s) * kxc, TILE), kxc), :]
                            for d in range(blocks)
                        ],
                        axis=0,
                    )
                    for s in range(2)
                ],
                axis=1,
            )
            high, low = split(both)
            result = dot(table_w[...], jnp.concatenate([high, high, low], axis=0))
            half[c, p] = result[:, :LANES]
            half[c, p + 1] = result[:, LANES:]

        send_h(c).start()
        keep_h(c).start()

    for copy in tables[:4]:
        copy.wait()
    pl.semaphore_wait(barrier, blocks)

    @pl.loop(0, chunks + AHEAD)
    def _(t):
        @pl.when(t < chunks)
        def _():
            density(t)

        @pl.when(t == AHEAD - 1)
        def _():
            prepare()

        c = t - AHEAD

        @pl.when(c >= 0)
        def _():
            spectrum(c)
            due = c - SLACK + 1

            @pl.when((due > 0) & (lax.rem(due + ratio * TILE, ratio) == 0) & (due // ratio < groups))
            def _():
                gather(due // ratio - 1)

    done = (chunks - SLACK) // ratio

    @pl.loop(max(done, 0), groups - 1)
    def _(g):
        gather(g)

    gather_last()
    filtered(0)

    @pl.loop(0, chunks)
    def _(c):
        @pl.when((lax.rem(c, ratio) == 0) & (c // ratio + 1 < groups))
        def _():
            filtered(c // ratio + 1)

        inverse(c)

    @pl.loop(0, chunks)
    def _(c):
        send_x(c).wait_send()
        arrivals(f_send.at[c]).wait()
        arrivals(b_send.at[c]).wait()
        send_h(c).wait_send()
        keep_h(c).wait()
        send_h(c).wait_recv()


def last_kernel(first, second, table, out):
    planes, nx, count = first.shape[1:]
    a, a_low = split(first[0].reshape(planes * nx, count))
    b, b_low = split(second[0].reshape(planes * nx, count))
    line = dot(jnp.concatenate([a, b, a_low, b_low, a, b], axis=1), table[...])
    out[...] = line.reshape(out.shape)


def fused(orbitals, kweights, occupations, z_basis, z_eigen):
    points, bands, parts, planes, nx, ny = orbitals.shape
    nz = z_basis.shape[0]
    blocks = lax.axis_size("grid")
    kxc = nx // blocks
    step = STEP
    chunks = planes // step
    groups = planes // TILE
    depth = blocks * TILE
    pairs = kxc // 2
    table_x, scaled_x = basis_tables(nx)
    table_y, scaled_y = basis_tables(ny)
    high, low = halves(table_y)
    stack = np.concatenate([high.T, high.T, low.T], axis=0)
    forward_y = np.stack([stack[:, :LANES], stack[:, LANES:]])
    high, low = halves(table_x)
    forward_x = np.concatenate([high, low, high], axis=1)
    high, low = halves(scaled_x.T)
    inverse_x = np.concatenate([high, low, high], axis=1)
    high, low = halves(scaled_y)
    inverse_y = np.concatenate([high, high, low], axis=0)
    wave_y = ((2.0 * np.sin(np.pi * np.arange(ny) / ny)) ** 2).astype(np.float32).reshape(2, LANES)
    wave_x = ((2.0 * np.sin(np.pi * np.arange(nx) / nx)) ** 2).astype(np.float32)

    anywhere = pl.BlockSpec(memory_space=pl.ANY)
    scalars = pl.BlockSpec(memory_space=pltpu.SMEM)
    vector = pl.BlockSpec(memory_space=pltpu.VMEM)
    dma = pltpu.SemaphoreType.DMA
    exchanged = pl.pallas_call(
        fused_kernel,
        out_shape=jax.ShapeDtypeStruct((2, planes, nx, LANES), f32),
        in_specs=[anywhere, scalars, scalars, anywhere, anywhere, anywhere, anywhere, anywhere, vector, scalars],
        out_specs=anywhere,
        scratch_shapes=[
            pltpu.VMEM((SLOTS, points, bands, parts, step, nx, ny), bf16),
            pltpu.VMEM((nx, 2 * ny), bf16),
            pltpu.VMEM((3 * ny, 2 * LANES), bf16),
            pltpu.VMEM((nx, 3 * nx), bf16),
            pltpu.VMEM((nx, 3 * nx), bf16),
            pltpu.VMEM((blocks, planes, nz), f32),
            pltpu.VMEM((1, nz), f32),
            pltpu.VMEM((chunks, step, nx, LANES), f32),
            pltpu.VMEM((chunks, step, nx, LANES), f32),
            pltpu.VMEM((chunks, step, nx, LANES), f32),
            pltpu.VMEM((planes * nx, LANES), f32),
            pltpu.VMEM((groups * depth * kxc, LANES), f32),
            pltpu.VMEM((pairs, nz, 2 * LANES), f32),
            pltpu.VMEM((pairs, nz, 2 * LANES), bf16),
            pltpu.VMEM((pairs, nz, 2 * LANES), bf16),
            pltpu.VMEM((groups, depth, nz), bf16),
            pltpu.VMEM((groups, depth, nz), bf16),
            pltpu.VMEM((groups, nz, 3 * depth), bf16),
            pltpu.VMEM((nz, LANES), f32),
            pltpu.VMEM((planes * nx, LANES), f32),
            pltpu.VMEM((chunks, step, nx, LANES), f32),
            dma((SLOTS,)),
            dma((6,)),
        ]
        + [dma((chunks,))] * 9,
        compiler_params=pltpu.CompilerParams(
            collective_id=0, has_side_effects=True, vmem_limit_bytes=62 * 1024 * 1024
        ),
        name="exchange",
    )(
        orbitals, kweights, occupations, z_basis.reshape(blocks, planes, nz), z_eigen.reshape(1, nz),
        jnp.asarray(forward_y), jnp.asarray(forward_x), jnp.asarray(inverse_x),
        jnp.asarray(wave_y), jnp.asarray(wave_x),
    )
    count = 4
    return pl.pallas_call(
        last_kernel,
        grid=(planes // count,),
        out_shape=jax.ShapeDtypeStruct((planes, nx, ny), f32),
        in_specs=[
            pl.BlockSpec((1, count, nx, LANES), lambda i: (0, i, 0, 0)),
            pl.BlockSpec((1, count, nx, LANES), lambda i: (1, i, 0, 0)),
            pl.BlockSpec((3 * ny, ny), lambda i: (0, 0)),
        ],
        out_specs=pl.BlockSpec((count, nx, ny), lambda i: (i, 0, 0)),
        name="last",
    )(exchanged, exchanged, jnp.asarray(inverse_y))


def real_basis(length):
    position = jnp.arange(length, dtype=jnp.int32)
    product = position[:, None] * position[None, :] % length
    angles = product.astype(jnp.float32) * (2.0 * jnp.pi / length)
    lower = position[:, None] <= length // 2
    table = jnp.where(lower, jnp.cos(angles), jnp.sin(angles))
    edges = (position == 0) | (position == length // 2)
    weights = jnp.where(edges, 1.0, 2.0).astype(jnp.float32) / length
    return (table, table * weights[:, None])


def on_device(orbitals, kweights, occupations, z_basis, z_eigen):
    points, band_count, _, planes, x_length, y_length = orbitals.shape
    z_length = z_basis.shape[0]
    groups = lax.axis_size("kpt")
    blocks = lax.axis_size("grid")
    group = lax.axis_index("kpt")
    ky_count = y_length // groups
    kx_count = x_length // blocks
    step = max(planes // CHUNKS, 1)
    chunks = planes // step
    factor = (kweights[:, None] * occupations).astype(jnp.float32) / (16.0 * points * band_count)
    table_x, scaled_x = real_basis(x_length)
    table_y, scaled_y = real_basis(y_length)

    def part_of(table, shift):
        start = lax.rem(group + shift, groups) * ky_count
        return lax.dynamic_slice_in_dim(table, start, ky_count, 0)

    def shifted_by(shift):
        return [(g, (g + shift) % groups) for g in range(groups)]

    forward_y = [part_of(table_y, shift) for shift in range(groups)]
    inverse_y = [part_of(scaled_y, shift) for shift in range(groups)]
    basis = z_basis.reshape(blocks, planes, z_length)

    projected = None
    for chunk in range(chunks):
        rows = slice(chunk * step, (chunk + 1) * step)
        values = orbitals[:, :, :, rows].astype(jnp.float32)
        density = jnp.sum(factor[:, :, None, None, None, None] * values * values, axis=(0, 1, 2))
        along = jnp.einsum("zxy,ky->zxk", density, forward_y[0], precision=precise)
        for shift in range(1, groups):
            other = jnp.einsum("zxy,ky->zxk", density, forward_y[shift], precision=precise)
            arrived = lax.ppermute(other, "kpt", shifted_by(shift))
            along = along + arrived
        spectrum = jnp.einsum("jx,zxk->zjk", table_x, along, precision=precise)
        column = lax.all_to_all(
            spectrum.reshape(step, blocks, kx_count, ky_count), "grid", split_axis=1, concat_axis=0, tiled=True
        ).reshape(blocks * step, kx_count, ky_count)
        z_rows = basis[:, rows].reshape(blocks * step, z_length)
        term = jnp.einsum("zj,zab->jab", z_rows, column, precision=precise)
        projected = term if projected is None else projected + term

    wave_x = (lax.axis_index("grid") * kx_count + jnp.arange(kx_count, dtype=jnp.int32)).astype(jnp.float32)
    wave_y = (group * ky_count + jnp.arange(ky_count, dtype=jnp.int32)).astype(jnp.float32)
    shift_x = 2.0 * jnp.sin(jnp.pi * wave_x / x_length)
    shift_y = 2.0 * jnp.sin(jnp.pi * wave_y / y_length)
    shifted = shift_x[:, None] ** 2 + shift_y[None, :] ** 2
    scaled = projected * (1.0 / (z_eigen[:, None, None] + shifted[None]))

    outputs = []
    for chunk in range(chunks):
        rows = slice(chunk * step, (chunk + 1) * step)
        z_rows = basis[:, rows].reshape(blocks * step, z_length)
        filtered = jnp.einsum("zj,jab->zab", z_rows, scaled, precision=precise)
        modes = lax.all_to_all(
            filtered.reshape(blocks, step, kx_count, ky_count), "grid", split_axis=0, concat_axis=0, tiled=True
        )
        half = jnp.einsum(
            "jx,zjk->zxk",
            scaled_x,
            modes.transpose(1, 0, 2, 3).reshape(step, x_length, ky_count),
            precision=precise,
        )
        total = jnp.einsum("zxk,ky->zxy", half, inverse_y[0], precision=precise)
        for shift in range(1, groups):
            arrived = lax.ppermute(half, "kpt", shifted_by(groups - shift))
            total = total + jnp.einsum("zxk,ky->zxy", arrived, inverse_y[shift], precision=precise)
        outputs.append(total)
    return jnp.concatenate(outputs, axis=0)


def solution(mesh):
    groups, blocks = mesh.shape["kpt"], mesh.shape["grid"]
    specs = dict(
        mesh=mesh,
        in_specs=(P("kpt", None, None, "grid", None, None), P("kpt"), P("kpt", None), P(), P()),
        out_specs=P("grid", None, None),
        check_vma=False,
    )
    plain = jax.shard_map(on_device, **specs)
    kernels = jax.shard_map(fused, **specs)

    def step(orbitals, *rest):
        _, _, _, nz, nx, ny = orbitals.shape
        fits = groups == 2 and ny == 2 * LANES and nx % (TILE * blocks) == 0 and nz % (TILE * blocks) == 0
        return (kernels if fits else plain)(orbitals, *rest)

    return step
```

profile of v0, /device:TPU:24, one launch (start us, length us, event | category | flops | bytes accessed | tf_op | source)
XLA Modules:
  0.0 238.6 jit_solution(4347848788054607529)
XLA Ops:
  0.0 227.9 %exchange.1.first.second = f32[2,32,256,128]{3,2,1,0:T(8,128)} custom-call(bf16[2,2,2,32,256,256]{5,4,3,2,1,0:T(8,128)(2,1)} %orbitals.1, s32[2]{0:T(128)} %kweights.1, s32[2,2]{1,0:T(2,128)} %occupations.1, f32[16,32,512]{2,1,0:T(8,128)} %bitcast.2, f32[1,512]{1,0:T(1,128)} %bitcast.3, bf16[2,768,128]{2,1,0:T(8,128)(2,1)} %constant.12.clone.forward_y, ...), custom_call_target="tpu_custom_call" | custom-call | tf_op jit(solution)/shard_map/exchange/pallas_call | solution.py:393
  227.9 10.7 %last.1 = f32[32,256,256]{2,1,0:T(8,128)} custom-call(f32[2,32,256,128]{3,2,1,0:T(8,128)} %exchange.1.first.second, f32[2,32,256,128]{3,2,1,0:T(8,128)} %exchange.1.first.second, bf16[768,256]{1,0:T(8,128)(2,1)} %constant.17.clone.table), custom_call_target="tpu_custom_call" | custom-call | tf_op jit(solution)/shard_map/last/pallas_call | solution.py:434
where the time goes:
time: 240 us; the launch traced here: 239 us
  Pallas kernels  239 us (100%)
    pallas_call x1, Pallas kernels, fused(): pl.pallas_call(fused_kernel, out_shape=jax.ShapeDtypeStruct((2, planes, n...  228 us
    pallas_call x1, Pallas kernels, fused(): pl.pallas_call(last_kernel, grid=(planes // count,), out_shape=jax.ShapeD...  10.7 us

commit v1 on v0

v1 whole, which is shorter than its diff:
```python
import jax
import jax.numpy as jnp
import numpy as np
from jax import lax
from jax.experimental import pallas as pl
from jax.experimental.pallas import tpu as pltpu
from jax.sharding import PartitionSpec as P


precise = lax.Precision.HIGH
CHUNKS = 4

MESH = pl.DeviceIdType.MESH
LANES = 128
TILE = 8
BITE = 2
STEP = 2
SLOTS = 3
LEAD = 3
PACE = 1
LATE = 4
EARLY = 2
WINDOW = 3
MIDDLE = 8
REST = 1
LATER = 4
bf16 = jnp.bfloat16
f32 = jnp.float32


def basis_tables(length):
    position = np.arange(length)
    angles = (position[:, None] * position[None, :] % length) * (2.0 * np.pi / length)
    table = np.where(position[:, None] <= length // 2, np.cos(angles), np.sin(angles))
    edges = (position == 0) | (position == length // 2)
    scaled = table * (np.where(edges, 1.0, 2.0) / length)[:, None]
    return table, scaled


def halves(table):
    high = table.astype(bf16)
    low = (table - high.astype(np.float64)).astype(bf16)
    return high, low


def split(value):
    high = value.astype(bf16)
    return high, (value - high.astype(f32)).astype(bf16)


def dot(left, right):
    return jnp.dot(left, right, preferred_element_type=f32)


def fused_kernel(
    orbitals, kweights, occupations, basis, eigen, forward_y, forward_x, inverse_x, wave_y, wave_x,
    line_out,
    block, rows, table_y, table_x, table_w, basis_rows, eigen_row, own, leaving, joined, column, projected,
    scaled_high, scaled_low, basis_high, basis_low, basis_turned, eigen_column, modes, others, line,
    load_sem, table_sem, x_send, x_recv, f_send, f_recv, b_send, b_recv, h_send, h_recv, keep_sem,
):
    points, bands, parts, planes, nx, ny = orbitals.shape
    blocks = lax.axis_size("grid")
    chunks = planes // STEP
    groups = planes // TILE
    ratio = TILE // STEP
    cuts = nx // (blocks * TILE)
    items = cuts * chunks
    depth = blocks * TILE
    pairs = TILE // 2
    share = STEP * TILE
    nz = basis.shape[0] * basis.shape[1]
    bites = planes // BITE
    per = STEP // BITE
    side = lax.axis_index("kpt")
    other = 1 - side
    me = lax.axis_index("grid")

    barrier = pltpu.get_barrier_semaphore()
    pl.semaphore_signal(barrier, inc=1, device_id={"kpt": other}, device_id_type=MESH)

    @pl.loop(1, blocks)
    def _(i):
        pl.semaphore_signal(barrier, inc=1, device_id={"grid": lax.rem(me + i, blocks)}, device_id_type=MESH)

    def load(b):
        slot = lax.rem(b, SLOTS)
        return pltpu.make_async_copy(
            orbitals.at[:, :, :, pl.ds(b * BITE, BITE)], block.at[slot], load_sem.at[slot]
        )

    load(0).start()
    tables = [
        pltpu.make_async_copy(forward_y.at[side], table_y, table_sem.at[0]),
        pltpu.make_async_copy(forward_x, table_x, table_sem.at[1]),
        pltpu.make_async_copy(inverse_x, table_w, table_sem.at[2]),
        pltpu.make_async_copy(basis, basis_rows, table_sem.at[3]),
        pltpu.make_async_copy(eigen, eigen_row, table_sem.at[4]),
    ]
    for copy in tables[:2]:
        copy.start()

    def part_of(e, d):
        return pl.ds(pl.multiple_of((e * blocks + d) * share, TILE), share)

    def place_of(e, d):
        c = lax.rem(e, chunks)
        first = ((e // chunks * groups + c // ratio) * blocks + d) * TILE + lax.rem(c, ratio) * STEP
        return pl.ds(pl.multiple_of(first * TILE, TILE), share)

    def whole_of(e):
        return pl.ds(pl.multiple_of(e * (blocks * share), TILE), blocks * share)

    def across_kpt(source, target, e, send, recv):
        return pltpu.make_async_remote_copy(
            src_ref=source.at[whole_of(e)], dst_ref=target.at[whole_of(e)],
            send_sem=send.at[e], recv_sem=recv.at[e], device_id={"kpt": other}, device_id_type=MESH,
        )

    def send_x(e):
        return across_kpt(leaving, joined, e, x_send, x_recv)

    def send_h(e):
        return across_kpt(modes, others, e, h_send, h_recv)

    def send_f(e, i):
        to = lax.rem(me + i, blocks)
        return pltpu.make_async_remote_copy(
            src_ref=own.at[part_of(e, to)], dst_ref=column.at[place_of(e, me)],
            send_sem=f_send.at[e], recv_sem=f_recv.at[e], device_id={"grid": to}, device_id_type=MESH,
        )

    def send_b(e, i):
        to = lax.rem(me + i, blocks)
        return pltpu.make_async_remote_copy(
            src_ref=column.at[place_of(e, to)], dst_ref=modes.at[part_of(e, me)],
            send_sem=b_send.at[e], recv_sem=b_recv.at[e], device_id={"grid": to}, device_id_type=MESH,
        )

    def arrivals(sem):
        whole = column.at[pl.ds(0, (blocks - 1) * share)]
        return pltpu.make_async_copy(whole, whole, sem)

    def density(b):
        slot = lax.rem(b, SLOTS)
        load(b).wait()

        @pl.when(b == 0)
        def _():
            for later in range(1, SLOTS):
                load(later).start()
            for copy in tables[2:]:
                copy.start()

        strip = 32
        factors = [
            [(kweights[k] * occupations[k, n]).astype(f32) / (16.0 * points * bands) for n in range(bands)]
            for k in range(points)
        ]

        @pl.loop(0, BITE * nx // strip)
        def _(r):
            p = r // (nx // strip)
            where = pl.ds(pl.multiple_of(lax.rem(r, nx // strip) * strip, strip), strip)
            target = pl.ds(pl.multiple_of(r * strip, strip), strip)
            total = None
            for k in range(points):
                for n in range(bands):
                    square = None
                    for part in range(parts):
                        value = block[slot, k, n, part, p, where, :].astype(f32)
                        square = value * value if square is None else square + value * value
                    term = factors[k][n] * square
                    total = term if total is None else total + term
            high, low = split(total)
            rows[target, pl.ds(0, ny)] = high
            rows[target, pl.ds(ny, ny)] = low

        @pl.when(b + SLOTS < bites)
        def _():
            load(b + SLOTS).start()

        along = dot(rows[...], table_y[pl.ds(0, 2 * ny), :]) + dot(
            rows[:, pl.ds(0, ny)], table_y[pl.ds(2 * ny, ny), :]
        )
        for p in range(BITE):
            high, low = split(along[p * nx : (p + 1) * nx])
            result = dot(table_x[...], jnp.concatenate([high, high, low], axis=0))
            c = b // per
            q = lax.rem(b, per) * BITE + p
            for h in range(cuts):
                for d in range(blocks):
                    first = (((h * chunks + c) * blocks + d) * STEP + q) * TILE
                    where = pl.ds(pl.multiple_of(first, TILE), TILE)
                    taken = result[(h * blocks + d) * TILE : (h * blocks + d + 1) * TILE]
                    leaving[where, :] = taken[:, :LANES]
                    own[where, :] = taken[:, LANES:]

    def spectrum(e):
        send_x(e).wait_recv()
        own[whole_of(e), :] += joined[whole_of(e), :]
        column[place_of(e, me), :] = own[part_of(e, me), :]

        @pl.when(e >= items - EARLY)
        def _():
            arrivals(f_recv.at[e - 1]).wait()

        @pl.loop(1, blocks)
        def _(i):
            send_f(e, i).start()

    def prepare():
        for copy in tables[2:]:
            copy.wait()

        @pl.loop(0, groups)
        def _(g):
            taken = basis_rows[:, pl.ds(pl.multiple_of(g * TILE, TILE), TILE), :].reshape(depth, nz)
            high, low = split(taken)
            basis_high[g] = high
            basis_low[g] = low
            high, low = split(taken.T)
            basis_turned[g, :, pl.ds(0, depth)] = high
            basis_turned[g, :, pl.ds(depth, depth)] = high
            basis_turned[g, :, pl.ds(2 * depth, depth)] = low

        eigen_column[...] = jnp.broadcast_to(eigen_row[...], (LANES, nz)).T

    def start_of(h, g, q):
        return (h * groups + g) * (depth * TILE) + 2 * q

    def term(h, g, q):
        start = start_of(h, g, q)
        both = jnp.concatenate(
            [column[pl.ds(start, depth, stride=TILE), :], column[pl.ds(start + 1, depth, stride=TILE), :]], axis=1
        )
        high, low = split(both)
        return dot(basis_turned[g], jnp.concatenate([high, low, high], axis=0))

    def wait_f(h, g):
        for r in range(ratio):
            e = h * chunks + g * ratio + r

            @pl.when((e < items - EARLY - 1) | (e == items - 1))
            def _():
                arrivals(f_recv.at[e]).wait()

    def gather(h, g):
        wait_f(h, g)

        @pl.loop(0, pairs)
        def _(q):
            projected[q] = jnp.where(g > 0, projected[q], 0.0) + term(h, g, q)

    def gather_last(h):
        g = groups - 1
        wait_f(h, g)
        across = wave_y[pl.ds(side, 1), :]

        @pl.loop(0, pairs)
        def _(q):
            total = term(h, g, q)
            if groups > 1:
                total = total + projected[q]
            for s in range(2):
                along = wave_x[(me * cuts + h) * TILE + 2 * q + s]
                value = total[:, s * LANES : (s + 1) * LANES] / (eigen_column[...] + (along + across))
                high, low = split(value)
                scaled_high[q, :, pl.ds(s * LANES, LANES)] = high
                scaled_low[q, :, pl.ds(s * LANES, LANES)] = low

    def filtered(h, g):
        @pl.loop(0, pairs)
        def _(q):
            result = (
                dot(basis_high[g], scaled_high[q])
                + dot(basis_high[g], scaled_low[q])
                + dot(basis_low[g], scaled_high[q])
            )
            start = start_of(h, g, q)
            column[pl.ds(start, depth, stride=TILE), :] = result[:, :LANES]
            column[pl.ds(start + 1, depth, stride=TILE), :] = result[:, LANES:]

        for r in range(ratio):
            e = h * chunks + g * ratio + r
            modes[part_of(e, me), :] = column[place_of(e, me), :]

    def give_back(e):
        @pl.loop(1, blocks)
        def _(i):
            send_b(e, i).start()

    def hand_over(e):
        arrivals(b_recv.at[e]).wait()
        send_h(e).start()

    def keep(c, s):
        slot = lax.rem(c, 2)
        return pltpu.make_async_copy(
            line.at[slot, s], line_out.at[side if s == 0 else other, pl.ds(c * STEP, STEP)], keep_sem.at[slot, s]
        )

    def inverse(c):
        for h in range(cuts):
            send_h(h * chunks + c).wait_recv()

        @pl.when(c >= 2)
        def _():
            for s in range(2):
                keep(c - 2, s).wait()

        slot = lax.rem(c, 2)

        @pl.loop(0, STEP)
        def _(p):
            both = jnp.concatenate(
                [
                    jnp.concatenate(
                        [
                            source[pl.ds(pl.multiple_of((((h * chunks + c) * blocks + d) * STEP + p) * TILE, TILE), TILE), :]
                            for h in range(cuts)
                            for d in range(blocks)
                        ],
                        axis=0,
                    )
                    for source in (modes, others)
                ],
                axis=1,
            )
            high, low = split(both)
            result = dot(table_w[...], jnp.concatenate([high, high, low], axis=0))
            line[slot, 0, p] = result[:, :LANES]
            line[slot, 1, p] = result[:, LANES:]

        for s in range(2):
            keep(c, s).start()

    for copy in tables[:2]:
        copy.wait()

    @pl.loop(0, bites)
    def _(b):
        density(b)

        @pl.when(b == 0)
        def _():
            pl.semaphore_wait(barrier, blocks)

        @pl.when(lax.rem(b, per) == per - 1)
        def _():
            send_x(b // per).start()

        @pl.when((b >= LEAD) & (lax.rem(b - LEAD, PACE) == 0))
        def _():
            spectrum((b - LEAD) // PACE)

    first = (bites - 1 - LEAD) // PACE + 1

    @pl.loop(chunks, items)
    def _(e):
        send_x(e).start()

    prepare()

    last = cuts - 1
    base = last * chunks + ratio + LATER - 1

    @pl.loop(first, items)
    def _(e):
        spectrum(e)
        at = chunks + LATE - groups

        @pl.when((e >= at) & (e < at + groups - 1))
        def _():
            gather(0, e - at)

        @pl.when(e == at + groups - 1)
        def _():
            gather_last(0)

        @pl.when((e >= at + groups) & (e < at + 2 * groups))
        def _():
            filtered(0, e - at - groups)

        @pl.when((e >= base) & (lax.rem(e - base + ratio * items, ratio) == 0))
        def _():
            gather(last, (e - base) // ratio)

        k = e - (items - EARLY)

        @pl.when(k >= 1)
        def _():
            hand_over(k - 1)

        @pl.when(k >= 0)
        def _():
            give_back(k)

    for e in range(EARLY, EARLY + WINDOW - 1):
        give_back(e)

    done = (items - 1 - base) // ratio + 1

    @pl.loop(EARLY - 1, items)
    def _(e):
        ahead = e + WINDOW
        hand_over(e)

        @pl.when(ahead < items)
        def _():
            give_back(ahead)

        @pl.when((e >= REST) & (e - REST + done < groups - 1))
        def _():
            gather(last, e - REST + done)

        @pl.when(e == MIDDLE)
        def _():
            gather_last(last)

        after = ahead + 1 - last * chunks

        @pl.when((after >= 0) & (after < chunks) & (lax.rem(after + items * ratio, ratio) == 0))
        def _():
            filtered(last, after // ratio)

        @pl.when(e > last * chunks)
        def _():
            inverse(e - last * chunks - 1)

    inverse(chunks - 1)

    for c in (chunks - 2, chunks - 1):
        for s in range(2):
            keep(c, s).wait()

    @pl.loop(0, items)
    def _(e):
        send_x(e).wait_send()
        arrivals(f_send.at[e]).wait()
        arrivals(b_send.at[e]).wait()
        send_h(e).wait_send()


def last_kernel(first, second, table, out):
    planes, nx, count = first.shape[1:]
    a, a_low = split(first[0].reshape(planes * nx, count))
    b, b_low = split(second[0].reshape(planes * nx, count))
    line = dot(jnp.concatenate([a, b, a_low, b_low, a, b], axis=1), table[...])
    out[...] = line.reshape(out.shape)


def fused(orbitals, kweights, occupations, z_basis, z_eigen):
    points, bands, parts, planes, nx, ny = orbitals.shape
    nz = z_basis.shape[0]
    blocks = lax.axis_size("grid")
    chunks = planes // STEP
    groups = planes // TILE
    cuts = nx // (blocks * TILE)
    items = cuts * chunks
    depth = blocks * TILE
    pairs = TILE // 2
    order = np.arange(nx).reshape(blocks, cuts, TILE).transpose(1, 0, 2).reshape(nx)
    table_x, scaled_x = basis_tables(nx)
    table_y, scaled_y = basis_tables(ny)
    high, low = halves(table_y)
    stack = np.concatenate([high.T, high.T, low.T], axis=0)
    forward_y = np.stack([np.roll(stack, LANES, axis=1), stack])
    high, low = halves(table_x[order])
    forward_x = np.concatenate([high, low, high], axis=1)
    high, low = halves(scaled_x[order].T)
    inverse_x = np.concatenate([high, low, high], axis=1)
    high, low = halves(scaled_y)
    inverse_y = np.concatenate([high, high, low], axis=0)
    wave_y = ((2.0 * np.sin(np.pi * np.arange(ny) / ny)) ** 2).astype(np.float32).reshape(2, LANES)
    wave_x = ((2.0 * np.sin(np.pi * np.arange(nx) / nx)) ** 2).astype(np.float32)

    anywhere = pl.BlockSpec(memory_space=pl.ANY)
    scalars = pl.BlockSpec(memory_space=pltpu.SMEM)
    vector = pl.BlockSpec(memory_space=pltpu.VMEM)
    dma = pltpu.SemaphoreType.DMA
    exchanged = pl.pallas_call(
        fused_kernel,
        out_shape=jax.ShapeDtypeStruct((2, planes, nx, LANES), f32),
        in_specs=[anywhere, scalars, scalars, anywhere, anywhere, anywhere, anywhere, anywhere, vector, scalars],
        out_specs=anywhere,
        scratch_shapes=[
            pltpu.VMEM((SLOTS, points, bands, parts, BITE, nx, ny), bf16),
            pltpu.VMEM((BITE * nx, 2 * ny), bf16),
            pltpu.VMEM((3 * ny, 2 * LANES), bf16),
            pltpu.VMEM((nx, 3 * nx), bf16),
            pltpu.VMEM((nx, 3 * nx), bf16),
            pltpu.VMEM((blocks, planes, nz), f32),
            pltpu.VMEM((1, nz), f32),
            pltpu.VMEM((planes * nx, LANES), f32),
            pltpu.VMEM((planes * nx, LANES), f32),
            pltpu.VMEM((planes * nx, LANES), f32),
            pltpu.VMEM((planes * nx, LANES), f32),
            pltpu.VMEM((pairs, nz, 2 * LANES), f32),
            pltpu.VMEM((pairs, nz, 2 * LANES), bf16),
            pltpu.VMEM((pairs, nz, 2 * LANES), bf16),
            pltpu.VMEM((groups, depth, nz), bf16),
            pltpu.VMEM((groups, depth, nz), bf16),
            pltpu.VMEM((groups, nz, 3 * depth), bf16),
            pltpu.VMEM((nz, LANES), f32),
            pltpu.VMEM((planes * nx, LANES), f32),
            pltpu.VMEM((planes * nx, LANES), f32),
            pltpu.VMEM((2, 2, STEP, nx, LANES), f32),
            dma((SLOTS,)),
            dma((5,)),
        ]
        + [dma((items,))] * 8
        + [dma((2, 2))],
        compiler_params=pltpu.CompilerParams(
            collective_id=0, has_side_effects=True, vmem_limit_bytes=62 * 1024 * 1024
        ),
        name="exchange",
    )(
        orbitals, kweights, occupations, z_basis.reshape(blocks, planes, nz), z_eigen.reshape(1, nz),
        jnp.asarray(forward_y), jnp.asarray(forward_x), jnp.asarray(inverse_x),
        jnp.asarray(wave_y), jnp.asarray(wave_x),
    )
    count = TILE
    return pl.pallas_call(
        last_kernel,
        grid=(planes // count,),
        out_shape=jax.ShapeDtypeStruct((planes, nx, ny), f32),
        in_specs=[
            pl.BlockSpec((1, count, nx, LANES), lambda i: (0, i, 0, 0)),
            pl.BlockSpec((1, count, nx, LANES), lambda i: (1, i, 0, 0)),
            pl.BlockSpec((3 * ny, ny), lambda i: (0, 0)),
        ],
        out_specs=pl.BlockSpec((count, nx, ny), lambda i: (i, 0, 0)),
        name="last",
    )(exchanged, exchanged, jnp.asarray(inverse_y))


def real_basis(length):
    position = jnp.arange(length, dtype=jnp.int32)
    product = position[:, None] * position[None, :] % length
    angles = product.astype(jnp.float32) * (2.0 * jnp.pi / length)
    lower = position[:, None] <= length // 2
    table = jnp.where(lower, jnp.cos(angles), jnp.sin(angles))
    edges = (position == 0) | (position == length // 2)
    weights = jnp.where(edges, 1.0, 2.0).astype(jnp.float32) / length
    return (table, table * weights[:, None])


def on_device(orbitals, kweights, occupations, z_basis, z_eigen):
    points, band_count, _, planes, x_length, y_length = orbitals.shape
    z_length = z_basis.shape[0]
    groups = lax.axis_size("kpt")
    blocks = lax.axis_size("grid")
    group = lax.axis_index("kpt")
    ky_count = y_length // groups
    kx_count = x_length // blocks
    step = max(planes // CHUNKS, 1)
    chunks = planes // step
    factor = (kweights[:, None] * occupations).astype(jnp.float32) / (16.0 * points * band_count)
    table_x, scaled_x = real_basis(x_length)
    table_y, scaled_y = real_basis(y_length)

    def part_of(table, shift):
        start = lax.rem(group + shift, groups) * ky_count
        return lax.dynamic_slice_in_dim(table, start, ky_count, 0)

    def shifted_by(shift):
        return [(g, (g + shift) % groups) for g in range(groups)]

    forward_y = [part_of(table_y, shift) for shift in range(groups)]
    inverse_y = [part_of(scaled_y, shift) for shift in range(groups)]
    basis = z_basis.reshape(blocks, planes, z_length)

    projected = None
    for chunk in range(chunks):
        rows = slice(chunk * step, (chunk + 1) * step)
        values = orbitals[:, :, :, rows].astype(jnp.float32)
        density = jnp.sum(factor[:, :, None, None, None, None] * values * values, axis=(0, 1, 2))
        along = jnp.einsum("zxy,ky->zxk", density, forward_y[0], precision=precise)
        for shift in range(1, groups):
            other = jnp.einsum("zxy,ky->zxk", density, forward_y[shift], precision=precise)
            arrived = lax.ppermute(other, "kpt", shifted_by(shift))
            along = along + arrived
        spectrum = jnp.einsum("jx,zxk->zjk", table_x, along, precision=precise)
        column = lax.all_to_all(
            spectrum.reshape(step, blocks, kx_count, ky_count), "grid", split_axis=1, concat_axis=0, tiled=True
        ).reshape(blocks * step, kx_count, ky_count)
        z_rows = basis[:, rows].reshape(blocks * step, z_length)
        term = jnp.einsum("zj,zab->jab", z_rows, column, precision=precise)
        projected = term if projected is None else projected + term

    wave_x = (lax.axis_index("grid") * kx_count + jnp.arange(kx_count, dtype=jnp.int32)).astype(jnp.float32)
    wave_y = (group * ky_count + jnp.arange(ky_count, dtype=jnp.int32)).astype(jnp.float32)
    shift_x = 2.0 * jnp.sin(jnp.pi * wave_x / x_length)
    shift_y = 2.0 * jnp.sin(jnp.pi * wave_y / y_length)
    shifted = shift_x[:, None] ** 2 + shift_y[None, :] ** 2
    scaled = projected * (1.0 / (z_eigen[:, None, None] + shifted[None]))

    outputs = []
    for chunk in range(chunks):
        rows = slice(chunk * step, (chunk + 1) * step)
        z_rows = basis[:, rows].reshape(blocks * step, z_length)
        filtered = jnp.einsum("zj,jab->zab", z_rows, scaled, precision=precise)
        modes = lax.all_to_all(
            filtered.reshape(blocks, step, kx_count, ky_count), "grid", split_axis=0, concat_axis=0, tiled=True
        )
        half = jnp.einsum(
            "jx,zjk->zxk",
            scaled_x,
            modes.transpose(1, 0, 2, 3).reshape(step, x_length, ky_count),
            precision=precise,
        )
        total = jnp.einsum("zxk,ky->zxy", half, inverse_y[0], precision=precise)
        for shift in range(1, groups):
            arrived = lax.ppermute(half, "kpt", shifted_by(groups - shift))
            total = total + jnp.einsum("zxk,ky->zxy", arrived, inverse_y[shift], precision=precise)
        outputs.append(total)
    return jnp.concatenate(outputs, axis=0)


def solution(mesh):
    groups, blocks = mesh.shape["kpt"], mesh.shape["grid"]
    specs = dict(
        mesh=mesh,
        in_specs=(P("kpt", None, None, "grid", None, None), P("kpt"), P("kpt", None), P(), P()),
        out_specs=P("grid", None, None),
        check_vma=False,
    )
    plain = jax.shard_map(on_device, **specs)
    kernels = jax.shard_map(fused, **specs)

    def step(orbitals, *rest):
        _, _, _, nz, nx, ny = orbitals.shape
        fits = groups == 2 and ny == 2 * LANES and nx == 2 * TILE * blocks and nz % (TILE * blocks) == 0
        return (kernels if fits else plain)(orbitals, *rest)

    return step
```

time: 240 us -> 218 us (0.908)
  Pallas kernels: 239 us -> 217 us
    pallas_call x1, Pallas kernels: 228 us -> 208 us  [fused(): pl.pallas_call(fused_kernel, out_shape=jax.ShapeDtypeStruct((2, planes, n...]
where the time goes in v1:
time: 218 us; the launch traced here: 217 us
  Pallas kernels  217 us (100%)
    pallas_call x1, Pallas kernels, fused(): pl.pallas_call(fused_kernel, out_shape=jax.ShapeDtypeStruct((2, planes, n...  208 us
    pallas_call x1, Pallas kernels, fused(): pl.pallas_call(last_kernel, grid=(planes // count,), out_shape=jax.ShapeD...  9.03 us

profile of v1, /device:TPU:24, one launch (start us, length us, event | category | flops | bytes accessed | tf_op | source)
XLA Modules:
  0.0 217.4 jit_solution(7698146731457802711)
XLA Ops:
  0.0 208.4 %exchange.1.first.second = f32[2,32,256,128]{3,2,1,0:T(8,128)} custom-call(bf16[2,2,2,32,256,256]{5,4,3,2,1,0:T(8,128)(2,1)} %orbitals.1, s32[2]{0:T(128)} %kweights.1, s32[2,2]{1,0:T(2,128)} %occupations.1, f32[16,32,512]{2,1,0:T(8,128)} %bitcast.2, f32[1,512]{1,0:T(1,128)} %bitcast.3, bf16[2,768,256]{2,1,0:T(8,128)(2,1)} %constant.12.clone.forward_y, ...), custom_call_target="tpu_custom_call" | custom-call | tf_op jit(solution)/shard_map/exchange/pallas_call | solution.py:482
  208.4 9.0 %last.1 = f32[32,256,256]{2,1,0:T(8,128)} custom-call(f32[2,32,256,128]{3,2,1,0:T(8,128)} %exchange.1.first.second, f32[2,32,256,128]{3,2,1,0:T(8,128)} %exchange.1.first.second, bf16[768,256]{1,0:T(8,128)(2,1)} %constant.17.clone.table), custom_call_target="tpu_custom_call" | custom-call | tf_op jit(solution)/shard_map/last/pallas_call | solution.py:524

commit v2 on v1

--- a/solution.py
+++ b/solution.py
@@ -14,6 +14,7 @@
 LANES = 128
 TILE = 8
 BITE = 2
+PART = 4
 STEP = 2
 SLOTS = 3
 LEAD = 3
@@ -442,12 +443,35 @@
         send_h(e).wait_send()
 
 
-def last_kernel(first, second, table, out):
-    planes, nx, count = first.shape[1:]
-    a, a_low = split(first[0].reshape(planes * nx, count))
-    b, b_low = split(second[0].reshape(planes * nx, count))
-    line = dot(jnp.concatenate([a, b, a_low, b_low, a, b], axis=1), table[...])
-    out[...] = line.reshape(out.shape)
+def last_kernel(lines, inverse_y, potential, given, made, table, in_sem, out_sem, table_sem):
+    planes, nx, ny = potential.shape
+
+    def take(i):
+        return pltpu.make_async_copy(lines.at[:, pl.ds(i * PART, PART)], given.at[i], in_sem.at[i])
+
+    def put(i):
+        return pltpu.make_async_copy(made.at[i], potential.at[pl.ds(i * PART, PART)], out_sem.at[i])
+
+    whole = pltpu.make_async_copy(inverse_y, table, table_sem)
+    whole.start()
+
+    @pl.loop(0, planes // PART)
+    def _(i):
+        take(i).start()
+
+    whole.wait()
+
+    @pl.loop(0, planes // PART)
+    def _(i):
+        take(i).wait()
+        both = [given[i, s].reshape(PART * nx, LANES) for s in range(2)]
+        high, low = split(jnp.concatenate(both, axis=1))
+        made[i] = dot(jnp.concatenate([high, low, high], axis=1), table[...]).reshape(PART, nx, ny)
+        put(i).start()
+
+    @pl.loop(0, planes // PART)
+    def _(i):
+        put(i).wait()
 
 
 def fused(orbitals, kweights, occupations, z_basis, z_eigen):
@@ -520,19 +544,23 @@
         jnp.asarray(forward_y), jnp.asarray(forward_x), jnp.asarray(inverse_x),
         jnp.asarray(wave_y), jnp.asarray(wave_x),
     )
-    count = TILE
+    counted = planes // PART
     return pl.pallas_call(
         last_kernel,
-        grid=(planes // count,),
         out_shape=jax.ShapeDtypeStruct((planes, nx, ny), f32),
-        in_specs=[
-            pl.BlockSpec((1, count, nx, LANES), lambda i: (0, i, 0, 0)),
-            pl.BlockSpec((1, count, nx, LANES), lambda i: (1, i, 0, 0)),
-            pl.BlockSpec((3 * ny, ny), lambda i: (0, 0)),
+        in_specs=[anywhere, anywhere],
+        out_specs=anywhere,
+        scratch_shapes=[
+            pltpu.VMEM((counted, 2, PART, nx, LANES), f32),
+            pltpu.VMEM((counted, PART, nx, ny), f32),
+            pltpu.VMEM((3 * ny, ny), bf16),
+            dma((counted,)),
+            dma((counted,)),
+            dma,
         ],
-        out_specs=pl.BlockSpec((count, nx, ny), lambda i: (i, 0, 0)),
+        compiler_params=pltpu.CompilerParams(vmem_limit_bytes=62 * 1024 * 1024),
         name="last",
-    )(exchanged, exchanged, jnp.asarray(inverse_y))
+    )(exchanged, jnp.asarray(inverse_y))
 
 
 def real_basis(length):

time: 218 us -> 216 us (level)
  no operation moved by 1% of the time
where the time goes in v2:
time: 216 us
  Pallas kernels  216 us (100%)
    pallas_call x1, Pallas kernels, fused(): pl.pallas_call(fused_kernel, out_shape=jax.ShapeDtypeStruct((2, planes, n...  208 us
    pallas_call x1, Pallas kernels, fused(): pl.pallas_call(last_kernel, out_shape=jax.ShapeDtypeStruct((planes, nx, n...  7.15 us

profile of v2, /device:TPU:24, one launch (start us, length us, event | category | flops | bytes accessed | tf_op | source)
XLA Modules:
  0.0 215.6 jit_solution(5309415330523039608)
XLA Ops:
  0.0 208.4 %exchange.1.lines = f32[2,32,256,128]{3,2,1,0:T(8,128)} custom-call(bf16[2,2,2,32,256,256]{5,4,3,2,1,0:T(8,128)(2,1)} %orbitals.1, s32[2]{0:T(128)} %kweights.1, s32[2,2]{1,0:T(2,128)} %occupations.1, f32[16,32,512]{2,1,0:T(8,128)} %bitcast.2, f32[1,512]{1,0:T(1,128)} %bitcast.3, bf16[2,768,256]{2,1,0:T(8,128)(2,1)} %constant.12.clone.forward_y, ...), custom_call_target="tpu_custom_call" | custom-call | tf_op jit(solution)/shard_map/exchange/pallas_call | solution.py:506
  208.4 7.2 %last.1 = f32[32,256,256]{2,1,0:T(8,128)} custom-call(f32[2,32,256,128]{3,2,1,0:T(8,128)} %exchange.1.lines, bf16[768,256]{1,0:T(8,128)(2,1)} %constant.17.clone.inverse_y), custom_call_target="tpu_custom_call" | custom-call | tf_op jit(solution)/shard_map/last/pallas_call | solution.py:548
